TPU v7x, 32 devices: a whole 2x2x4 slice. The times are simulated.
32 devices in a mesh: dp: 4 (over z), expert: 8 (over y, x, core).
Axes of the slice: x: 2, y: 2, z: 4, core: 2. Of those that a mesh axis runs over, the one named last changes fastest.
Arguments:
- grad_output: bfloat16 [8, 8, 3840], P('expert', None, 'dp'), may hold values from -6 to 6
- router_logits: float32 [8, 8, 32], P('expert'), may hold values from -8 to 8
- expert_ids: int32 [8, 8, 8], P('expert'), may hold values from 0 to 31, all different within a row; in each aligned block of 8 rows (0 to 7, 8 to 15, ..., all dimensions but the last counted through in order) at most 3 rows name the same one
- router_input: bfloat16 [8, 8, 3840], P('expert', 'dp'), may hold values from -6 to 6
- router_weight: bfloat16 [32, 3840], P(None, 'dp'), may hold values from -0.09375 to 0.09375
- gate_weight: bfloat16 [32, 3840, 1024], P('expert', 'dp'), may hold values from -0.09375 to 0.09375
- up_weight: bfloat16 [32, 3840, 1024], P('expert', 'dp'), may hold values from -0.09375 to 0.09375
- down_weight: bfloat16 [32, 1024, 3840], P('expert', None, 'dp'), may hold values from -0.1875 to 0.1875
- gate_saved: bfloat16 [32, 24, 1024], P('expert'), may hold values from -6 to 6
- up_saved: bfloat16 [32, 24, 1024], P('expert'), may hold values from -6 to 6
Outputs:
- grad_input: bfloat16 [8, 8, 3840], P('expert', None, 'dp')
- grad_router: float32 [32, 3840], P('expert', 'dp')
Inputs may be any that keep to these rules, and one draw needn't show every extreme that they name: `expert_ids`: within one token group (the 8 tokens of one index of expert, in order), no expert is named more than 3 times, a bound that some block reaches; every row names 8 different experts.
All inputs are finite; a program needn't handle non-finite values.
Results may differ from a plain program's by a relative error of at most 0.008.
Values may be sent and summed in bfloat16 or wider, within the bound.
No kernel may reach another device: no remote copies, remote signals or barrier semaphores. Data moves between devices by JAX's collectives and lax.ppermute only.
A program may use at most 64 MiB of HBM per device.

v0:
```python
import jax
import jax.numpy as jnp
from jax import lax
from jax.sharding import PartitionSpec as P

route_scale = 2.5


def split_pair(values):
    upper = values.astype(jnp.bfloat16)
    lower = (values - upper.astype(jnp.float32)).astype(jnp.bfloat16)
    return jnp.stack([upper, lower], axis=-1)


def join_pair(paired):
    return paired[..., 0].astype(jnp.float32) + paired[..., 1].astype(jnp.float32)


def activation_backward(hidden_grad, saved_gate, saved_up):
    gate_value = saved_gate.astype(jnp.float32)
    up_value = saved_up.astype(jnp.float32)
    gate_sigmoid = jax.nn.sigmoid(gate_value)
    activated = gate_value * gate_sigmoid
    hidden = lax.optimization_barrier((activated * up_value).astype(jnp.bfloat16)).astype(
        jnp.float32
    )
    gate_share = jnp.sum(hidden * hidden_grad, axis=1)
    gate_part = (
        hidden_grad * up_value * gate_sigmoid * (1.0 + gate_value * (1.0 - gate_sigmoid))
    ).astype(jnp.bfloat16)
    up_part = (hidden_grad * activated).astype(jnp.bfloat16)
    return (gate_part, up_part, gate_share)


def local(
    grad_output,
    router_logits,
    expert_ids,
    router_input,
    router_weight,
    gate_weight,
    up_weight,
    down_weight,
    gate_saved,
    up_saved,
):
    expert_count = lax.axis_size("expert")
    out_rows = grad_output[0]
    group_size, feature_share = out_rows.shape
    expert_total = router_logits.shape[2]
    top_count = expert_ids.shape[2]
    local_experts, slot_count, hidden_size = gate_saved.shape
    slot_depth = slot_count // expert_count
    assign_count = group_size * top_count
    flat_ids = expert_ids[0].reshape(assign_count)
    expert_hot = (flat_ids[:, None] == jnp.arange(expert_total, dtype=jnp.int32)[None, :]).astype(
        jnp.int32
    )
    earlier = jnp.cumsum(expert_hot, axis=0) - expert_hot
    ranking = jnp.sum(expert_hot * earlier, axis=1)
    target = flat_ids * slot_depth + ranking
    slot_place = (
        jnp.arange(expert_total * slot_depth, dtype=jnp.int32)[:, None] == target[None, :]
    ).astype(jnp.bfloat16)
    owner_hot = (
        (jnp.arange(assign_count, dtype=jnp.int32) // top_count)[:, None]
        == jnp.arange(group_size, dtype=jnp.int32)[None, :]
    ).astype(jnp.bfloat16)
    slot_token = jnp.dot(slot_place, owner_hot, preferred_element_type=jnp.float32).astype(
        jnp.bfloat16
    )
    outgoing = jnp.dot(slot_token, out_rows, preferred_element_type=jnp.float32).astype(
        jnp.bfloat16
    )
    incoming = lax.all_to_all(
        outgoing.reshape(expert_total, slot_depth, feature_share),
        "expert",
        split_axis=0,
        concat_axis=1,
        tiled=True,
    )
    partial_hidden = jnp.einsum(
        "esd,efd->esf", incoming, down_weight, preferred_element_type=jnp.float32
    )
    row_total = local_experts * slot_count
    hidden_grad = lax.psum(partial_hidden.reshape(row_total, hidden_size), "dp")
    grad_gate, grad_up, gate_grad = activation_backward(
        hidden_grad,
        gate_saved.reshape(row_total, hidden_size),
        up_saved.reshape(row_total, hidden_size),
    )
    grad_gate = grad_gate.reshape(local_experts, slot_count, hidden_size)
    grad_up = grad_up.reshape(local_experts, slot_count, hidden_size)
    gate_grad = gate_grad.reshape(local_experts, slot_count)
    expert_input = jnp.einsum(
        "esf,edf->esd", grad_gate, gate_weight, preferred_element_type=jnp.float32
    )
    expert_input = expert_input + jnp.einsum(
        "esf,edf->esd", grad_up, up_weight, preferred_element_type=jnp.float32
    )
    expert_input = expert_input.astype(jnp.bfloat16)
    rows_back, gate_paired_back = (
        lax.all_to_all(expert_input, "expert", split_axis=1, concat_axis=0, tiled=True),
        lax.all_to_all(split_pair(gate_grad), "expert", split_axis=1, concat_axis=0, tiled=True),
    )
    gate_back = join_pair(gate_paired_back)
    pick_map = slot_place.T.astype(jnp.float32)
    picked_gate = jnp.dot(
        pick_map, gate_back.reshape(expert_total * slot_depth), precision=lax.Precision.HIGHEST
    ).reshape(group_size, top_count)
    scores = jax.nn.sigmoid(router_logits[0])
    hot_float = expert_hot.reshape(group_size, top_count, expert_total).astype(jnp.float32)
    chosen = jnp.sum(hot_float * scores[:, None, :], axis=2)
    chosen_total = jnp.sum(chosen, axis=1, keepdims=True)
    gates = route_scale * chosen / chosen_total
    mixture = jnp.sum(picked_gate * gates, axis=1, keepdims=True)
    d_chosen = (route_scale * picked_gate - mixture) / chosen_total
    d_scores = jnp.sum(hot_float * d_chosen[:, :, None], axis=1)
    logit_grad = (d_scores * scores * (1.0 - scores)).astype(jnp.bfloat16)
    grouped_input = lax.all_to_all(router_input[0], "dp", split_axis=1, concat_axis=0, tiled=True)
    router_term = jnp.einsum(
        "ge,gc->ec", logit_grad, grouped_input, preferred_element_type=jnp.float32
    )
    grad_router = lax.psum_scatter(router_term, "expert", scatter_dimension=0, tiled=True)
    picked_rows = jnp.dot(
        slot_place.T,
        rows_back.reshape(expert_total * slot_depth, feature_share),
        preferred_element_type=jnp.float32,
    )
    mixed = jnp.sum(
        gates[:, :, None] * picked_rows.reshape(group_size, top_count, feature_share), axis=1
    )
    router_part = jnp.dot(logit_grad, router_weight, preferred_element_type=jnp.float32)
    grad_input = (mixed + router_part).astype(jnp.bfloat16)[None]
    return (grad_input, grad_router)


def solution(mesh):
    placed = (
        P("expert", None, "dp"),
        P("expert", None, None),
        P("expert", None, None),
        P("expert", "dp", None),
        P(None, "dp"),
        P("expert", "dp", None),
        P("expert", "dp", None),
        P("expert", None, "dp"),
        P("expert", None, None),
        P("expert", None, None),
    )
    return jax.shard_map(
        local,
        mesh=mesh,
        in_specs=placed,
        out_specs=(P("expert", None, "dp"), P("expert", "dp")),
        check_vma=False,
    )
```

profile of v0, /device:TPU:0, one launch (start us, length us, event | category | flops | bytes accessed | tf_op | source)
XLA Modules:
  0.0 147.4 jit_solution(7802566168627807311)
XLA Ops:
  7.2 0.0 copy-start
  7.2 0.0 copy-start.3
  7.2 0.0 copy-start.4
  7.2 0.0 copy-start.1
  7.2 0.0 copy-start.2
  7.2 0.8 reshape_squeeze.3
  8.1 0.1 fusion.14
  8.1 0.1 reduce_window_sum.11
  8.2 0.2 select_reduce_fusion
  8.4 1.2 convolution_convert_fusion
  9.7 0.8 reshape.186
  10.5 5.2 %all-to-all-start = ((bf16[32,3,960]{2,1,0:T(4,128)(2,1)}), bf16[32,3,960]{2,1,0:T(4,128)(2,1)S(1)}, u32[]{:S(2)}, u32[]{:S(2)}) async-start(bf16[32,3,960]{2,1,0:T(4,128)(2,1)} %reshape.186), calls=%async_computation | async-start | bytes 524288 | tf_op jit(solution)/shard_map/all_to_all | solution.py:75
  15.7 0.8 all_to_all.62
  16.5 0.6 copy.46
  17.1 5.5 %all-to-all-done = bf16[32,3,960]{2,1,0:T(4,128)(2,1)S(1)} async-done(((bf16[32,3,960]{2,1,0:T(4,128)(2,1)}), bf16[32,3,960]{2,1,0:T(4,128)(2,1)S(1)}, u32[]{:S(2)}, u32[]{:S(2)}) %all-to-all-start) | async-done | bytes 184352 | tf_op jit(solution)/shard_map/all_to_all | solution.py:75
  22.6 4.9 %all-to-all-start.3 = ((bf16[2,4,960]{2,0,1:T(2,128)(2,1)}), bf16[2,4,960]{2,0,1:T(2,128)(2,1)S(1)}, u32[]{:S(2)}, u32[]{:S(2)}) async-start(bf16[2,4,960]{2,0,1:T(2,128)(2,1)} %copy.46), calls=%async_computation.3 | async-start | bytes 32768 | tf_op jit(solution)/shard_map/all_to_all | solution.py:120
  27.5 0.0 all-reduce.4.cloned.1.call-start
  27.5 0.1 copy.38
  27.6 5.1 %fusion.12 = f32[4,24,1024]{2,1,0:T(8,128)} fusion(bf16[4,1024,960]{1,2,0:T(8,128)(2,1)} %param.17, bf16[4,24,960]{2,0,1:T(4,128)(2,1)S(1)} %bitcast.79), kind=kOutput, calls=%fused_computation.24 | convolution fusion | flops 188743680 | bytes 8441856 | tf_op jit(solution)/shard_map/esd,efd->esf/dot_general | solution.py:82
  32.7 0.0 all-reduce.4.cloned.1.call-update
  32.7 0.0 copy-done.4
  32.8 0.1 reduce_sum.71
  32.8 0.0 copy-done.3
  32.9 0.2 fusion.15
  33.1 0.0 all-to-all-done.3
  33.1 36.3 %all-reduce.4.cloned.1.call-done = f32[96,1024]{1,0:T(8,128)} async-done(((f32[96,1024]{1,0:T(8,128)}), f32[96,1024]{1,0:T(8,128)}) %all-reduce.4.cloned.1.call-update) | async-done | bytes 393232 | tf_op jit(solution)/shard_map/psum | solution.py:86
  69.4 0.0 copy-done.1
  69.4 0.0 copy-done.2
  69.4 1.2 multiply_convert_fusion
  70.7 1.1 multiply_reduce_fusion
  71.8 0.1 reshape.191
  71.9 0.7 copy.42
  72.6 3.6 %all-to-all-start.2 = ((bf16[4,24,2]{0,2,1:T(2,128)(2,1)}), bf16[4,24,2]{0,2,1:T(2,128)(2,1)S(1)}, u32[]{:S(2)}, u32[]{:S(2)}) async-start(bf16[4,24,2]{0,2,1:T(2,128)(2,1)} %copy.42), calls=%async_computation.2 | async-start | bytes 24576 | tf_op jit(solution)/shard_map/all_to_all | solution.py:104
  76.2 0.0 all-reduce.6.cloned.1.call-start
  76.2 0.0 copy-start.5
  76.3 5.4 %fusion.41 = f32[4,24,960]{2,1,0:T(8,128)S(1)} fusion(bf16[4,24,1024]{2,1,0:T(8,128)(2,1)S(1)} %bitcast.81, bf16[4,960,1024]{2,1,0:T(8,128)(2,1)} %param.15), kind=kOutput, calls=%fused_computation.74 | convolution fusion | flops 188743680 | bytes 8429568 | tf_op jit(solution)/shard_map/esf,edf->esd/dot_general | solution.py:95
  81.6 0.0 all-to-all-done.2
  81.7 0.1 all_to_all.61
  81.8 0.1 copy.45
  81.9 0.1 reshape.195
  82.0 0.4 fusion.20
  82.4 0.2 multiply_reduce_fusion.2
  82.6 0.1 subtract_divide_fusion
  82.6 0.1 multiply_reduce_fusion.1
  82.8 0.9 fusion.32
  83.6 0.0 all-reduce.6.cloned.1.call-update
  83.7 5.4 %fusion = bf16[4,24,960]{2,1,0:T(8,128)(2,1)S(1)} fusion(f32[4,24,960]{2,1,0:T(8,128)S(1)} %fusion.41, bf16[4,24,1024]{2,1,0:T(8,128)(2,1)S(1)} %bitcast.80, bf16[4,960,1024]{2,1,0:T(8,128)(2,1)} %param.16), kind=kOutput, calls=%fused_computation.1 | convolution fusion | flops 188928000 | bytes 8613888 | tf_op jit(solution)/shard_map/esf,edf->esd/dot_general | solution.py:98
  89.0 0.8 copy.40
  89.9 4.2 %all-to-all-start.1 = ((bf16[4,24,960]{2,0,1:T(4,128)(2,1)}), bf16[4,24,960]{2,0,1:T(4,128)(2,1)S(1)}, u32[]{:S(2)}, u32[]{:S(2)}) async-start(bf16[4,24,960]{2,0,1:T(4,128)(2,1)} %copy.40), calls=%async_computation.1 | async-start | bytes 393216 | tf_op jit(solution)/shard_map/all_to_all | solution.py:103
  94.0 0.0 copy-done.5
  94.0 0.6 dynamic-slice
  95.3 42.5 %all-reduce.6.cloned.1.call-done = f32[32,960]{1,0:T(8,128)} async-done(((f32[32,960]{1,0:T(8,128)}), f32[32,960]{1,0:T(8,128)}) %all-reduce.6.cloned.1.call-update) | async-done | bytes 122896
  137.8 1.4 constant_dynamic-slice_fusion
  139.2 0.0 all-to-all-done.1
  139.2 0.1 copy.41
  139.3 0.2 reshape.194
  139.5 0.3 fusion.1
  139.8 0.0 copy-done
  139.8 0.7 fusion.3
  (8 shorter events, 0.1 us)
Async XLA Ops:
  7.2 132.6 %copy-start = (bf16[32,960]{1,0:T(8,128)(2,1)S(1)}, bf16[32,960]{1,0:T(8,128)(2,1)}, u32[]{:S(2)}) copy-start(bf16[32,960]{1,0:T(8,128)(2,1)} %param.14) | copy-start | bytes 184324
  7.2 25.7 %copy-start.3 = (s32[1,8,8]{2,1,0:T(8,128)S(1)}, s32[1,8,8]{2,1,0:T(8,128)}, u32[]{:S(2)}) copy-start(s32[1,8,8]{2,1,0:T(8,128)} %param.12) | copy-start | bytes 772
  7.2 25.6 %copy-start.4 = (f32[1,8,32]{2,1,0:T(8,128)S(1)}, f32[1,8,32]{2,1,0:T(8,128)}, u32[]{:S(2)}) copy-start(f32[1,8,32]{2,1,0:T(8,128)} %param.11) | copy-start | bytes 3076
  7.2 62.2 %copy-start.1 = (bf16[4,24,1024]{2,1,0:T(8,128)(2,1)S(1)}, bf16[4,24,1024]{2,1,0:T(8,128)(2,1)}, u32[]{:S(2)}) copy-start(bf16[4,24,1024]{2,1,0:T(8,128)(2,1)} %param.18) | copy-start | bytes 589828
  7.2 62.2 %copy-start.2 = (bf16[4,24,1024]{2,1,0:T(8,128)(2,1)S(1)}, bf16[4,24,1024]{2,1,0:T(8,128)(2,1)}, u32[]{:S(2)}) copy-start(bf16[4,24,1024]{2,1,0:T(8,128)(2,1)} %param.19) | copy-start | bytes 589828
  10.5 12.1 %all-to-all-start = ((bf16[32,3,960]{2,1,0:T(4,128)(2,1)}), bf16[32,3,960]{2,1,0:T(4,128)(2,1)S(1)}, u32[]{:S(2)}, u32[]{:S(2)}) async-start(bf16[32,3,960]{2,1,0:T(4,128)(2,1)} %reshape.186), calls=%async_computation | async-start | bytes 524288 | tf_op jit(solution)/shard_map/all_to_all | solution.py:75
  22.6 10.5 %all-to-all-start.3 = ((bf16[2,4,960]{2,0,1:T(2,128)(2,1)}), bf16[2,4,960]{2,0,1:T(2,128)(2,1)S(1)}, u32[]{:S(2)}, u32[]{:S(2)}) async-start(bf16[2,4,960]{2,0,1:T(2,128)(2,1)} %copy.46), calls=%async_computation.3 | async-start | bytes 32768 | tf_op jit(solution)/shard_map/all_to_all | solution.py:120
  27.5 42.0 %all-reduce.4.cloned.1.call-start = ((), (), s32[]{:S(2)}) async-start(), calls=%async_computation.4 | async-start | bytes 786432 | tf_op jit(solution)/shard_map/psum | solution.py:86
  72.6 9.0 %all-to-all-start.2 = ((bf16[4,24,2]{0,2,1:T(2,128)(2,1)}), bf16[4,24,2]{0,2,1:T(2,128)(2,1)S(1)}, u32[]{:S(2)}, u32[]{:S(2)}) async-start(bf16[4,24,2]{0,2,1:T(2,128)(2,1)} %copy.42), calls=%async_computation.2 | async-start | bytes 24576 | tf_op jit(solution)/shard_map/all_to_all | solution.py:104
  76.2 61.6 %all-reduce.6.cloned.1.call-start = ((), (), s32[]{:S(2)}) async-start(), calls=%async_computation.5 | async-start | bytes 262144
  76.2 17.8 %copy-start.5 = (u32[32]{0:T(128)S(1)}, u32[32]{0:T(128)}, u32[]{:S(2)}) copy-start(u32[32]{0:T(128)} %constant.42) | copy-start | bytes 388
  89.9 49.3 %all-to-all-start.1 = ((bf16[4,24,960]{2,0,1:T(4,128)(2,1)}), bf16[4,24,960]{2,0,1:T(4,128)(2,1)S(1)}, u32[]{:S(2)}, u32[]{:S(2)}) async-start(bf16[4,24,960]{2,0,1:T(4,128)(2,1)} %copy.40), calls=%async_computation.1 | async-start | bytes 393216 | tf_op jit(solution)/shard_map/all_to_all | solution.py:103
Sparse Core Ops, SparseCore 0:
  32.9 36.5 all-reduce.3
  83.8 53.9 all-reduce.5
where the time goes:
time: 148 us; the launch traced here: 147 us
  waiting for transfers between devices  84.4 us (57%)
  matrix products  19.4 us (13%)
  starting transfers between devices  17.8 us (12%)
  between operations  14.9 us (10%)
  local copies, waits for them, and re-layouts  7.53 us (5%)
  other arithmetic  3.35 us (2%)
    unnamed x3, waiting for transfers between devices  42.5 us
    psum x1, waiting for transfers between devices, local(): hidden_grad = lax.psum(partial_hidden.reshape(row_total, hidden_size), 'dp')  36.3 us
    all_to_all x1, waiting for transfers between devices, local(): lax.all_to_all(outgoing.reshape(expert_total, slot_depth, feature_share),...  5.47 us
    dot_general x1, matrix products, local(): jnp.einsum('esf,edf->esd', grad_up, up_weight, preferred_element_type=jnp...  5.39 us
    dot_general x1, matrix products, local(): jnp.einsum('esf,edf->esd', grad_gate, gate_weight, preferred_element_type...  5.39 us
    all_to_all x1, starting transfers between devices, local(): lax.all_to_all(outgoing.reshape(expert_total, slot_depth, feature_share),...  5.2 us
    dot_general x1, matrix products, local(): jnp.einsum('esd,efd->esf', incoming, down_weight, preferred_element_type=...  5.13 us
    all_to_all x1, starting transfers between devices, local(): lax.all_to_all(router_input[0], 'dp', split_axis=1, concat_axis=0, tiled=...  4.87 us
  transfers between devices with their start and end apart: 6, of which 3 were waited for; matrix products, arithmetic and copies ran while one was open for 13% of the time, Pallas kernels for 0%

commit v1 on v0

--- a/solution.py
+++ b/solution.py
@@ -83,7 +83,9 @@
         "esd,efd->esf", incoming, down_weight, preferred_element_type=jnp.float32
     )
     row_total = local_experts * slot_count
-    hidden_grad = lax.psum(partial_hidden.reshape(row_total, hidden_size), "dp")
+    hidden_grad = jnp.sum(
+        lax.all_gather(partial_hidden.reshape(row_total, hidden_size), "dp"), axis=0
+    )
     grad_gate, grad_up, gate_grad = activation_backward(
         hidden_grad,
         gate_saved.reshape(row_total, hidden_size),

time: 148 us -> 140 us (0.946)
  waiting for transfers between devices: 84.4 us -> 72 us
  blocking collectives: 0 us -> 11.9 us
  starting transfers between devices: 17.8 us -> 12.7 us
    psum x1 -> x0, waiting for transfers between devices: 36.3 us -> none  [local(): hidden_grad = lax.psum(partial_hidden.reshape(row_total, hidden_size), 'dp')]
    all_gather x0 -> x1, waiting for transfers between devices: none -> 25.2 us  [local(): lax.all_gather(partial_hidden.reshape(row_total, hidden_size), 'dp')]
    all_to_all x0 -> x1, blocking collectives: none -> 11.9 us  [local(): lax.all_to_all(outgoing.reshape(expert_total, slot_depth, feature_share),...]
    all_to_all x1 -> x0, waiting for transfers between devices: 5.47 us -> none  [local(): lax.all_to_all(outgoing.reshape(expert_total, slot_depth, feature_share),...]
    all_to_all x1, waiting for transfers between devices: 0.01 us -> 5.33 us  [local(): lax.all_to_all(router_input[0], 'dp', split_axis=1, concat_axis=0, tiled=...]
    all_to_all x1 -> x0, starting transfers between devices: 5.2 us -> none  [local(): lax.all_to_all(outgoing.reshape(expert_total, slot_depth, feature_share),...]
    reduce_sum x0 -> x1, other arithmetic: none -> 1.55 us  [local(): jnp.sum(lax.all_gather(partial_hidden.reshape(row_total, hidden_size), 'd...]
  transfers between devices with their start and end apart: 6 -> 5, of which waited for: 3 -> 3; matrix products, arithmetic and copies ran while one was open for 13% -> 10% of each run, Pallas kernels for 0% -> 0%
where the time goes in v1:
time: 140 us
  waiting for transfers between devices  72 us (51%)
  matrix products  19.4 us (14%)
  between operations  14.9 us (11%)
  starting transfers between devices  12.7 us (9%)
  blocking collectives  11.9 us (8%)
  local copies, waits for them, and re-layouts  6.2 us (4%)
  other arithmetic  2.78 us (2%)
    unnamed x3, waiting for transfers between devices  41.4 us
    all_gather x1, waiting for transfers between devices, local(): lax.all_gather(partial_hidden.reshape(row_total, hidden_size), 'dp')  25.2 us
    all_to_all x1, blocking collectives, local(): lax.all_to_all(outgoing.reshape(expert_total, slot_depth, feature_share),...  11.9 us
    dot_general x1, matrix products, local(): jnp.einsum('esf,edf->esd', grad_gate, gate_weight, preferred_element_type...  5.39 us
    dot_general x1, matrix products, local(): jnp.einsum('esf,edf->esd', grad_up, up_weight, preferred_element_type=jnp...  5.39 us
    all_to_all x1, waiting for transfers between devices, local(): lax.all_to_all(router_input[0], 'dp', split_axis=1, concat_axis=0, tiled=...  5.33 us
    dot_general x1, matrix products, local(): jnp.einsum('esd,efd->esf', incoming, down_weight, preferred_element_type=...  5.12 us
    all_to_all x1, starting transfers between devices, local(): lax.all_to_all(router_input[0], 'dp', split_axis=1, concat_axis=0, tiled=...  4.87 us
  transfers between devices with their start and end apart: 5, of which 3 were waited for; matrix products, arithmetic and copies ran while one was open for 10% of the time, Pallas kernels for 0%

profile of v1, /device:TPU:0, one launch (start us, length us, event | category | flops | bytes accessed | tf_op | source)
XLA Modules:
  0.0 139.8 jit_solution(8428201138624496408)
XLA Ops:
  7.2 0.0 copy-start
  7.2 0.0 copy-start.3
  7.2 0.0 copy-start.5
  7.2 0.0 copy-start.4
  7.2 0.0 copy-start.1
  7.2 0.0 copy-start.2
  7.2 0.0 all-gather.2.cloned.1.call-start
  7.3 0.9 reshape_squeeze.3
  8.2 0.1 fusion.24
  8.3 0.1 reduce_window_sum.11
  8.4 0.2 select_reduce_fusion
  8.5 1.2 convolution_convert_fusion
  9.8 0.1 reshape.181
  9.9 11.9 %all_to_all.70 = bf16[32,3,960]{2,1,0:T(4,128)(2,1)S(1)} all-to-all(bf16[32,3,960]{2,1,0:T(4,128)(2,1)S(1)} %reshape.181), channel_id=1, replica_groups=mesh['dp'=4,'expert'=8] {'expert'}, dimensions={0} | all-to-all | bytes 368640 | tf_op jit(solution)/shard_map/all_to_all | solution.py:75
  21.8 0.1 copy.38
  21.9 5.1 %fusion.19 = f32[4,24,1024]{2,1,0:T(8,128)} fusion(bf16[4,1024,960]{1,2,0:T(8,128)(2,1)} %param.17, bf16[4,24,960]{2,0,1:T(4,128)(2,1)S(1)} %bitcast.83), kind=kOutput, calls=%fused_computation.29 | convolution fusion | flops 188743680 | bytes 8441856 | tf_op jit(solution)/shard_map/esd,efd->esf/dot_general | solution.py:82
  27.1 0.0 all-gather.2.cloned.1.call-update
  27.1 0.0 copy-done.5
  27.1 0.1 all_to_all.62
  27.2 0.6 copy.46
  27.8 4.9 %all-to-all-start.3 = ((bf16[2,4,960]{2,0,1:T(2,128)(2,1)}), bf16[2,4,960]{2,0,1:T(2,128)(2,1)S(1)}, u32[]{:S(2)}, u32[]{:S(2)}) async-start(bf16[2,4,960]{2,0,1:T(2,128)(2,1)} %copy.46), calls=%async_computation.3 | async-start | bytes 32768 | tf_op jit(solution)/shard_map/all_to_all | solution.py:122
  32.7 0.1 reduce_sum.84
  32.8 0.0 copy-done.4
  32.8 0.0 copy-done.3
  32.8 0.0 copy-done.1
  32.8 0.0 copy-done.2
  32.8 0.1 fusion.4
  33.0 0.2 fusion.25
  33.2 5.3 %all-to-all-done.3 = bf16[2,4,960]{2,0,1:T(2,128)(2,1)S(1)} async-done(((bf16[2,4,960]{2,0,1:T(2,128)(2,1)}), bf16[2,4,960]{2,0,1:T(2,128)(2,1)S(1)}, u32[]{:S(2)}, u32[]{:S(2)}) %all-to-all-start.3) | async-done | bytes 15392 | tf_op jit(solution)/shard_map/all_to_all | solution.py:122
  38.5 25.2 %all-gather.2.cloned.1.call-done = f32[4,96,1024]{2,1,0:T(8,128)} async-done(((f32[1,96,1024]{2,1,0:T(8,128)}), f32[4,96,1024]{2,1,0:T(8,128)}) %all-gather.2.cloned.1.call-update) | async-done | bytes 1572880 | tf_op jit(solution)/shard_map/all_gather | solution.py:87
  63.7 1.6 %reduce_sum.81 = f32[96,1024]{1,0:T(8,128)S(1)} reduce(f32[4,96,1024]{2,1,0:T(8,128)} %all-gather.2.cloned.1.call-done, f32[]{:T(128)} %constant.24.clone.1), dimensions={0}, to_apply=%region_4.5 | reduce | flops 294912 | bytes 1966084 | tf_op jit(solution)/shard_map/reduce_sum | solution.py:86
  65.3 0.1 multiply_reduce_fusion
  65.4 0.1 reshape.183
  65.5 0.7 copy.42
  66.2 3.6 %all-to-all-start.2 = ((bf16[4,24,2]{0,2,1:T(2,128)(2,1)}), bf16[4,24,2]{0,2,1:T(2,128)(2,1)S(1)}, u32[]{:S(2)}, u32[]{:S(2)}) async-start(bf16[4,24,2]{0,2,1:T(2,128)(2,1)} %copy.42), calls=%async_computation.2 | async-start | bytes 24576 | tf_op jit(solution)/shard_map/all_to_all | solution.py:106
  69.8 0.0 all-reduce.3.cloned.1.call-start
  69.8 0.0 copy-start.6
  69.9 5.4 %fusion.17 = f32[4,24,960]{2,1,0:T(8,128)S(1)} fusion(bf16[4,960,1024]{2,1,0:T(8,128)(2,1)} %param.15, bf16[4,24,1024]{2,1,0:T(8,128)(2,1)S(1)} %copy-done.1, f32[4,24,1024]{2,1,0:T(8,128)S(1)} %bitcast.78, bf16[4,24,1024]{2,1,0:T(8,128)(2,1)S(1)} %copy-done.2), kind=kOutput, calls=%fused_computation.28 | convolution fusion | flops 189923328 | bytes 9019392 | tf_op jit(solution)/shard_map/esf,edf->esd/dot_general | solution.py:97
  75.2 0.0 all-to-all-done.2
  75.3 0.1 all_to_all.61
  75.4 0.1 copy.45
  75.5 0.1 reshape.187
  75.6 0.4 fusion.30
  76.0 0.2 multiply_reduce_fusion.2
  76.2 0.1 subtract_divide_fusion
  76.2 0.1 multiply_reduce_fusion.1
  76.4 0.9 fusion.42
  77.2 0.0 all-reduce.3.cloned.1.call-update
  77.3 5.4 %fusion = bf16[4,24,960]{2,1,0:T(8,128)(2,1)S(1)} fusion(f32[4,24,960]{2,1,0:T(8,128)S(1)} %fusion.17, bf16[4,960,1024]{2,1,0:T(8,128)(2,1)} %param.16, f32[4,24,1024]{2,1,0:T(8,128)S(1)} %bitcast.79, bf16[4,24,1024]{2,1,0:T(8,128)(2,1)S(1)} %copy-done.1), kind=kOutput, calls=%fused_computation.1 | convolution fusion | flops 189616128 | bytes 9007104 | tf_op jit(solution)/shard_map/esf,edf->esd/dot_general | solution.py:100
  82.6 0.8 copy.40
  83.5 4.2 %all-to-all-start.1 = ((bf16[4,24,960]{2,0,1:T(4,128)(2,1)}), bf16[4,24,960]{2,0,1:T(4,128)(2,1)S(1)}, u32[]{:S(2)}, u32[]{:S(2)}) async-start(bf16[4,24,960]{2,0,1:T(4,128)(2,1)} %copy.40), calls=%async_computation.1 | async-start | bytes 393216 | tf_op jit(solution)/shard_map/all_to_all | solution.py:105
  87.6 0.0 copy-done.6
  87.6 0.6 dynamic-slice
  88.9 41.4 %all-reduce.3.cloned.1.call-done = f32[32,960]{1,0:T(8,128)} async-done(((f32[32,960]{1,0:T(8,128)}), f32[32,960]{1,0:T(8,128)}) %all-reduce.3.cloned.1.call-update) | async-done | bytes 122896
  130.3 1.4 constant_dynamic-slice_fusion
  131.6 0.0 all-to-all-done.1
  131.6 0.1 copy.41
  131.8 0.2 reshape.186
  132.0 0.3 fusion.1
  132.2 0.0 copy-done
  132.2 0.7 fusion.3
  (8 shorter events, 0.1 us)
Async XLA Ops:
  7.2 125.1 %copy-start = (bf16[32,960]{1,0:T(8,128)(2,1)S(1)}, bf16[32,960]{1,0:T(8,128)(2,1)}, u32[]{:S(2)}) copy-start(bf16[32,960]{1,0:T(8,128)(2,1)} %param.14) | copy-start | bytes 184324
  7.2 25.6 %copy-start.3 = (s32[1,8,8]{2,1,0:T(8,128)S(1)}, s32[1,8,8]{2,1,0:T(8,128)}, u32[]{:S(2)}) copy-start(s32[1,8,8]{2,1,0:T(8,128)} %param.12) | copy-start | bytes 772
  7.2 19.9 %copy-start.5 = (bf16[1,2,3840]{2,1,0:T(2,128)(2,1)S(1)}, bf16[1,2,3840]{2,1,0:T(2,128)(2,1)}, u32[]{:S(2)}) copy-start(bf16[1,2,3840]{2,1,0:T(2,128)(2,1)} %param.13) | copy-start | bytes 46084
  7.2 25.6 %copy-start.4 = (f32[1,8,32]{2,1,0:T(8,128)S(1)}, f32[1,8,32]{2,1,0:T(8,128)}, u32[]{:S(2)}) copy-start(f32[1,8,32]{2,1,0:T(8,128)} %param.11) | copy-start | bytes 3076
  7.2 25.6 %copy-start.1 = (bf16[4,24,1024]{2,1,0:T(8,128)(2,1)S(1)}, bf16[4,24,1024]{2,1,0:T(8,128)(2,1)}, u32[]{:S(2)}) copy-start(bf16[4,24,1024]{2,1,0:T(8,128)(2,1)} %param.18) | copy-start | bytes 589828
  7.2 25.6 %copy-start.2 = (bf16[4,24,1024]{2,1,0:T(8,128)(2,1)S(1)}, bf16[4,24,1024]{2,1,0:T(8,128)(2,1)}, u32[]{:S(2)}) copy-start(bf16[4,24,1024]{2,1,0:T(8,128)(2,1)} %param.19) | copy-start | bytes 589828
  7.2 56.5 %all-gather.2.cloned.1.call-start = ((), (), s32[]{:S(2)}) async-start(), calls=%async_computation.4 | async-start | bytes 1966080 | tf_op jit(solution)/shard_map/all_gather | solution.py:87
  27.8 10.7 %all-to-all-start.3 = ((bf16[2,4,960]{2,0,1:T(2,128)(2,1)}), bf16[2,4,960]{2,0,1:T(2,128)(2,1)S(1)}, u32[]{:S(2)}, u32[]{:S(2)}) async-start(bf16[2,4,960]{2,0,1:T(2,128)(2,1)} %copy.46), calls=%async_computation.3 | async-start | bytes 32768 | tf_op jit(solution)/shard_map/all_to_all | solution.py:122
  66.2 9.0 %all-to-all-start.2 = ((bf16[4,24,2]{0,2,1:T(2,128)(2,1)}), bf16[4,24,2]{0,2,1:T(2,128)(2,1)S(1)}, u32[]{:S(2)}, u32[]{:S(2)}) async-start(bf16[4,24,2]{0,2,1:T(2,128)(2,1)} %copy.42), calls=%async_computation.2 | async-start | bytes 24576 | tf_op jit(solution)/shard_map/all_to_all | solution.py:106
  69.8 60.5 %all-reduce.3.cloned.1.call-start = ((), (), s32[]{:S(2)}) async-start(), calls=%async_computation.5 | async-start | bytes 262144
  69.8 17.8 %copy-start.6 = (u32[32]{0:T(128)S(1)}, u32[32]{0:T(128)}, u32[]{:S(2)}) copy-start(u32[32]{0:T(128)} %constant.42) | copy-start | bytes 388
  83.5 48.2 %all-to-all-start.1 = ((bf16[4,24,960]{2,0,1:T(4,128)(2,1)}), bf16[4,24,960]{2,0,1:T(4,128)(2,1)S(1)}, u32[]{:S(2)}, u32[]{:S(2)}) async-start(bf16[4,24,960]{2,0,1:T(4,128)(2,1)} %copy.40), calls=%async_computation.1 | async-start | bytes 393216 | tf_op jit(solution)/shard_map/all_to_all | solution.py:105
Sparse Core Ops, SparseCore 0:
  27.2 36.4 all-gather.1
  77.4 52.8 all-reduce.2
